TPU v7x, 256 devices: a whole 4x4x8 slice. The times are simulated.
256 devices in a mesh: row: 16 (over x, y), col: 16 (over z, core).
Axes of the slice: x: 4, y: 4, z: 8, core: 2. Of those that a mesh axis runs over, the one named last changes fastest.
Arguments:
- values: bfloat16 [8192, 8192], P('row', 'col'), may hold values from 0.0001296997 to 0.12988281
- tile_mask: int32 [64, 64], P('row', 'col'), may hold values 0 or 1
- keep_mask: int32 [64, 64], P('row', 'col'), may hold values 0 or 1
- thr_index: int32 [8192], P('col'), may hold values from 0 to 9
Outputs:
- expanded: bfloat16 [8192, 8192], P('row', 'col')
All inputs are finite; a program needn't handle non-finite values. No bound on the sum of `tile_mask` or of `keep_mask` on one device may be relied on, other than what follows from the above.
Results may differ from a plain program's by a relative error of at most 0.0004.
Values may be sent and summed in bfloat16 or wider, within the bound.
A program may use at most 64 MiB of HBM per device.

v0:
```python
import functools

import jax
import jax.numpy as jnp
from jax import lax
from jax.experimental import pallas as pl
from jax.experimental.pallas import tpu as pltpu
from jax.sharding import PartitionSpec as P

TB = 128
CORES = 2
CHUNKS = 4


def snake(index, width):
    line, spot = index // width, index % width
    return line * width + spot + (line % 2) * (width - 1 - 2 * spot)


def kernel(
    row_dev, col_dev, width, chunks, order,
    v_ref, tile_ref, keep_ref, thr_ref, acc, totals_ref,
    row_panel, col_panel, sums, stats,
    line_send, line_recv, pair_send, pair_recv, ring_send, ring_recv,
    sum_send, sum_recv, stat_send, stat_recv, loaded, load_sem, token,
):
    rows, cols = v_ref.shape
    step_rows = rows // chunks
    chips = col_dev // CORES
    half = row_dev // 2
    me_row, me_col = lax.axis_index("row"), lax.axis_index("col")
    z, core = me_col // CORES, me_col % CORES
    pos = snake(me_row, width)

    def ring_device(offset):
        return snake((pos + offset + row_dev) % row_dev, width)

    barrier = pltpu.get_barrier_semaphore()
    pl.semaphore_signal(barrier, inc=1, device_id={"col": z * CORES + 1 - core})
    peers = 1 + (z > 0).astype(jnp.int32) + (z < chips - 1).astype(jnp.int32)
    for offset in ((1, -1) if row_dev > 2 else (1,) * half):
        pl.semaphore_signal(barrier, inc=1, device_id={"row": ring_device(offset)})
        peers += 1

    @pl.when(z > 0)
    def _():
        pl.semaphore_signal(barrier, inc=1, device_id={"col": me_col - CORES})

    @pl.when(z < chips - 1)
    def _():
        pl.semaphore_signal(barrier, inc=1, device_id={"col": me_col + CORES})

    def load(q):
        spot = pl.ds(q * step_rows, step_rows)
        return pltpu.make_async_copy(v_ref.at[spot], loaded.at[spot], load_sem.at[q])

    for q in range(chunks):
        load(q).start()

    stored = tile_ref[...].astype(jnp.float32)
    kept = keep_ref[...].astype(jnp.float32)
    height = min(step_rows, TB)
    for lo in range(0, rows, height):
        if lo % step_rows == 0:
            load(lo // step_rows).wait()
        for b in range(cols // TB):
            r, c = slice(lo, lo + height), slice(b * TB, (b + 1) * TB)
            scale = jnp.broadcast_to(stored[b : b + 1, lo // TB : lo // TB + 1], (height, TB))
            tile = (loaded[r, c].astype(jnp.float32) * scale).astype(jnp.bfloat16)
            row_panel[me_col, r, c] = tile
            col_panel[pl.ds(pl.multiple_of(me_row * rows + lo, height), height), c] = tile

    pl.semaphore_wait(barrier, peers)

    def row_part(block, q):
        return row_panel.at[block, pl.ds(q * step_rows, step_rows)]

    def line_copy(zi, q, to_right):
        part = row_part(zi * CORES + core, q)
        return pltpu.make_async_remote_copy(
            src_ref=part, dst_ref=part,
            send_sem=line_send.at[to_right, zi, q], recv_sem=line_recv.at[zi, q],
            device_id={"col": me_col + (CORES if to_right else -CORES)},
        )

    def pair_copy(zi, q, lane):
        part = row_part(zi * CORES + lane, q)
        return pltpu.make_async_remote_copy(
            src_ref=part, dst_ref=part,
            send_sem=pair_send.at[zi, q], recv_sem=pair_recv.at[zi, q],
            device_id={"col": z * CORES + 1 - core},
        )

    def ring_copy(owner, q, to_right):
        start = pl.multiple_of(owner * rows + q * step_rows, step_rows)
        part = col_panel.at[pl.ds(start, step_rows)]
        return pltpu.make_async_remote_copy(
            src_ref=part, dst_ref=part,
            send_sem=ring_send.at[to_right, owner, q], recv_sem=ring_recv.at[owner, q],
            device_id={"row": ring_device(1 if to_right else -1)},
        )

    def on_ring(d, q, to_right):
        if d < half:
            return True
        return d == half and (q < chunks // 2) == bool(to_right)

    def relay(zi, q, to_right, wait):
        if wait:
            line_copy(zi, q, to_right).wait_recv()
        go = (z < chips - 1) if to_right else (z > 0)

        @pl.when(go)
        def _():
            line_copy(zi, q, to_right).start()

    for q in range(chunks):
        for to_right in (1, 0):
            relay(z, q, to_right, False)
            if on_ring(1, q, to_right):
                ring_copy(me_row, q, to_right).start()
        pair_copy(z, q, core).start()

    for to_right in (1, 0):
        first, end = (0, chips - 1) if to_right else (chips - 1, 0)

        @pl.when(z != first)
        def _():
            pl.semaphore_wait(token.at[to_right], 1)

        @pl.when(z != end)
        def _():
            pl.semaphore_signal(
                token.at[to_right], inc=1,
                device_id={"col": me_col + (CORES if to_right else -CORES)},
            )

    def line_step(t, q):
        for to_right in (1, 0):
            valid = (z >= t) if to_right else (z + t < chips)
            zi = z - t if to_right else z + t
            if t < chips:
                @pl.when(valid)
                def _():
                    relay(zi, q, to_right, True)
                    pair_copy(zi, q, core).start()

    def ring_step(t, q):
        for to_right in (1, 0):
            if on_ring(t, q, to_right):
                owner = ring_device(-t if to_right else t)
                ring_copy(owner, q, to_right).wait_recv()
                if on_ring(t + 1, q, to_right):
                    ring_copy(owner, q, to_right).start()

    def stat_copy(d):
        return pltpu.make_async_remote_copy(
            src_ref=stats.at[0], dst_ref=stats.at[d],
            send_sem=stat_send.at[d], recv_sem=stat_recv.at[d],
            device_id={"col": (me_col + d) % col_dev},
        )

    def send_stats():
        total = jnp.zeros((1, cols), jnp.float32)
        for i in range(row_dev):
            block = col_panel[i * rows : (i + 1) * rows].astype(jnp.float32)
            total += jnp.sum(block, axis=0, keepdims=True)
        stats[0] = total
        for d in range(1, col_dev):
            stat_copy(d).start()

    def product_sums():
        total = jnp.zeros((1, cols), jnp.float32)
        for d in range(col_dev):
            if d:
                stat_copy(d).wait()
            block = (me_col - d + col_dev) % col_dev
            inner = pl.ds(pl.multiple_of(block * cols, cols), cols)
            rest, terms = stats[d], []
            for _ in range(3):
                term = rest.astype(jnp.bfloat16).astype(jnp.float32)
                rest = rest - term
                terms.append(jnp.broadcast_to(term, (8, cols)))
            spread = jnp.dot(
                jnp.concatenate(terms, axis=0).astype(jnp.bfloat16), col_panel[inner],
                preferred_element_type=jnp.float32,
            )
            total += spread[16:17] + spread[8:9] + spread[0:1]
        return total

    def compute(zi, q, first=False):
        spot = pl.ds(pl.multiple_of(q * step_rows, step_rows), step_rows)
        total = None
        for lane in range(CORES):
            block = zi * CORES + lane
            inner = pl.ds(pl.multiple_of(block * cols, cols), cols)
            term = jnp.dot(
                row_panel[block, spot], col_panel[inner], preferred_element_type=jnp.float32
            )
            total = term if total is None else total + term
        if first:
            acc[spot] = total
        else:
            acc[spot] += total

    def take(zi, q, first=False):
        pair_copy(zi, q, 1 - core).wait_recv()
        compute(zi, q, first)

    def sides(t):
        return ((z >= t, z - t), (z + t < chips, z + t))

    def bulk(upto):
        @pl.loop(0, chunks)
        def _(q):
            take(z, q, True)
            for t in range(1, min(upto, chips - 1) + 1):
                for valid, zi in sides(t):
                    @pl.when(valid)
                    def _():
                        take(zi, q)

    def prune(q, cut):
        parts = []
        for b in range(cols // TB):
            c = slice(b * TB, (b + 1) * TB)
            part = jnp.zeros((1, TB), jnp.float32)
            for lo in range(q * step_rows, (q + 1) * step_rows, min(step_rows, TB)):
                r = slice(lo, lo + min(step_rows, TB))
                keep = jnp.broadcast_to(kept[b : b + 1, lo // TB : lo // TB + 1], (r.stop - lo, TB))
                pruned = jnp.maximum(acc[r, c] - cut[:, c], 0.0) * keep
                acc[r, c] = pruned
                part += jnp.sum(pruned, axis=0, keepdims=True)
            parts.append(part)
        return jnp.concatenate(parts, axis=1)

    def cuts():
        return 0.125 * thr_ref[...].astype(jnp.float32) * (product_sums() / order)

    part = jnp.zeros((1, cols), jnp.float32)
    last = max(chips - 1, half)
    if half == 0:
        send_stats()
        bulk(0)
    for t in range(1, last + 1):
        if t == half:
            for q in range(chunks):
                ring_step(t, q)
            send_stats()
            for q in range(chunks):
                line_step(t, q)
            bulk(t)
        else:
            if t == last and t > half:
                cut = cuts()
            for q in range(chunks):
                line_step(t, q)
                if t < half:
                    ring_step(t, q)
                else:
                    for valid, zi in sides(t):
                        @pl.when(valid)
                        def _():
                            take(zi, q)
                    if t == last:
                        part += prune(q, cut)
    if last <= half:
        cut = cuts()
        for q in range(chunks):
            part += prune(q, cut)

    sums[0] = part

    def sum_copy(d):
        return pltpu.make_async_remote_copy(
            src_ref=sums.at[0], dst_ref=sums.at[d],
            send_sem=sum_send.at[d], recv_sem=sum_recv.at[d],
            device_id={"row": (me_row + d) % row_dev},
        )

    for d in range(1, row_dev):
        sum_copy(d).start()
    for d in range(1, row_dev):
        sum_copy(d).wait()
        part += sums[d]
    totals_ref[...] = 1.0 / jnp.maximum(part / order, 0.1)

    for q in range(chunks):
        for zi in range(chips):
            pair_copy(zi, q, core).wait_send()

            @pl.when((z < chips - 1) & (z >= zi))
            def _():
                line_copy(zi, q, 1).wait_send()

            @pl.when((z > 0) & (z <= zi))
            def _():
                line_copy(zi, q, 0).wait_send()
        for d in range(0, half):
            for to_right in (1, 0):
                if on_ring(d + 1, q, to_right):
                    owner = ring_device(-d if to_right else d)
                    ring_copy(owner, q, to_right).wait_send()


def on_device(values, tile_mask, keep_mask, thr_index, *, row_dev, col_dev):
    rows, cols = values.shape
    width = max(w for w in range(1, row_dev + 1) if row_dev % w == 0 and w * w <= row_dev)
    chips = col_dev // CORES
    dma = pltpu.SemaphoreType.DMA
    vmem = pl.BlockSpec(memory_space=pltpu.VMEM)
    pruned, scale = pl.pallas_call(
        functools.partial(kernel, row_dev, col_dev, width, CHUNKS, rows * row_dev),
        out_shape=(
            pltpu.VMEM((rows, cols), jnp.float32),
            jax.ShapeDtypeStruct((1, cols), jnp.float32),
        ),
        in_specs=[pl.BlockSpec(memory_space=pl.ANY)] + [vmem] * 3,
        out_specs=(vmem, vmem),
        scratch_shapes=[
            pltpu.VMEM((col_dev, rows, cols), jnp.bfloat16),
            pltpu.VMEM((row_dev * rows, cols), jnp.bfloat16),
            pltpu.VMEM((row_dev, 1, cols), jnp.float32),
            pltpu.VMEM((col_dev, 1, cols), jnp.float32),
            dma((2, chips, CHUNKS)),
            dma((chips, CHUNKS)),
            dma((chips, CHUNKS)),
            dma((chips, CHUNKS)),
            dma((2, row_dev, CHUNKS)),
            dma((row_dev, CHUNKS)),
            dma((row_dev,)),
            dma((row_dev,)),
            dma((col_dev,)),
            dma((col_dev,)),
            pltpu.VMEM((rows, cols), jnp.bfloat16),
            dma((CHUNKS,)),
            pltpu.SemaphoreType.REGULAR((2,)),
        ],
        compiler_params=pltpu.CompilerParams(
            collective_id=0, has_side_effects=True,
            vmem_limit_bytes=63 * 2**20 - 4 * rows * cols + 2**19,
        ),
    )(values, tile_mask.T, keep_mask.T, thr_index.reshape(1, cols))
    return (pruned * scale).astype(jnp.bfloat16)


def solution(mesh):
    return jax.shard_map(
        functools.partial(on_device, row_dev=mesh.shape["row"], col_dev=mesh.shape["col"]),
        mesh=mesh,
        in_specs=(P("row", "col"), P("row", "col"), P("row", "col"), P("col")),
        out_specs=P("row", "col"),
        check_vma=False,
    )
```

profile of v0, /device:TPU:8, one launch (start us, length us, event | category | flops | bytes accessed | tf_op | source)
XLA Modules:
  0.0 121.1 jit_solution(12612424355302661058)
XLA Ops:
  0.0 0.0 copy-start.1
  0.0 1.4 %copy.5 = s32[4,4]{0,1:T(4,128)} copy(s32[4,4]{1,0:T(4,128)} %param.5) | data formatting | bytes 128 | tf_op args[1]
  1.4 0.0 copy-done.1
  1.4 0.7 copy.6
  2.0 117.5 %shard_map.46 = (f32[512,512]{1,0:T(8,128)S(1)}, f32[1,512]{1,0:T(1,128)}) custom-call(bf16[512,512]{1,0:T(8,128)(2,1)} %v_ref.1, s32[4,4]{1,0:T(4,128)} %bitcast.4, s32[4,4]{1,0:T(4,128)} %bitcast.5, s32[1,512]{1,0:T(1,128)} %bitcast.6), custom_call_target="tpu_custom_call" | custom-call | tf_op jit(solution)/shard_map/pallas_call | solution.py:312
  119.5 0.0 copy-start
  119.5 0.6 copy-done
  120.2 0.9 multiply_convert_fusion
Async XLA Ops:
  0.0 1.4 %copy-start.1 = (s32[4,4]{1,0:T(4,128)S(1)}, s32[4,4]{1,0:T(4,128)}, u32[]{:S(2)}) copy-start(s32[4,4]{1,0:T(4,128)} %param.6) | copy-start | bytes 196
  119.5 0.7 copy-start
where the time goes:
time: 121 us
  Pallas kernels  117 us (97%)
  local copies, waits for them, and re-layouts  2.66 us (2%)
    pallas_call x1, Pallas kernels, on_device(): pl.pallas_call(functools.partial(kernel, row_dev, col_dev, width, CHUNKS,...  117 us
    unnamed x6, local copies, waits for them, and re-layouts  2.66 us

commit v1 on v0

v1 whole, which is shorter than its diff:
```python
import functools

import jax
import jax.numpy as jnp
from jax import lax
from jax.experimental import pallas as pl
from jax.experimental.pallas import tpu as pltpu
from jax.sharding import PartitionSpec as P

TB = 128
CORES = 2
SIDE = 4
CHIPS = 8
CHUNKS = 4
LAST = 10
EXTRA = 16
LINKS = ((1, 0), (-1, 0), (0, 1), (0, -1))

ORDER = (
    ((0, 0), (1, 0), (2, 0), (3, 0), (0, 4), (2, 3), (3, 3), (2, 4), (2, 1), (3, 1), (2, 2), (3, 2), (2, 5), (2, 7), (2, 6)),
    ((1, 0), (0, 0), (3, 0), (2, 0), (1, 12), (3, 1), (2, 1), (3, 12), (3, 3), (2, 3), (3, 2), (2, 2), (3, 13), (3, 15), (3, 14)),
    ((2, 0), (3, 0), (0, 0), (1, 0), (2, 1), (0, 12), (1, 12), (0, 4), (0, 1), (1, 4), (0, 8), (0, 13), (1, 8), (0, 5), (0, 9)),
    ((3, 0), (2, 0), (1, 0), (0, 0), (3, 3), (1, 4), (0, 4), (1, 12), (1, 3), (0, 12), (1, 8), (1, 15), (1, 7), (0, 8), (1, 11)),
)
SLOTS = len(ORDER[0])
Z_ORDER = (
    tuple((c, 0) for c in (0, 1, 2, 3)) + tuple((c, 1) for c in (0, 1, 2, 3))
    + tuple((c, 2) for c in (0, 1, 2, 3)) + ((0, 3), (1, 3)),
    tuple((c, 0) for c in (2, 3, 0, 1)) + tuple((c, 1) for c in (2, 3, 0, 1))
    + tuple((c, 2) for c in (2, 3, 0, 1)) + ((2, 3), (3, 3)),
)
Z_SLOTS = len(Z_ORDER[0])
AHEAD = 3
POINTS = (7, 9, 11, 12, 13)


def shift(place, link):
    dx, dy = LINKS[link]
    return (place // SIDE + dx) % SIDE * SIDE + (place % SIDE + dy) % SIDE


def arrivals():
    xy = {(c, shift(p, n)): s for n in range(4) for s, (c, p) in enumerate(ORDER[n])}
    z = {}
    for n, sign in ((0, 1), (1, -1)):
        for s, (c, hop) in enumerate(Z_ORDER[n]):
            z[c, sign * (hop + 1) % CHIPS] = s
    return xy, z


XY_AT, Z_AT = arrivals()
BLOCK_AT = {p: max(XY_AT[c, p] for c in range(CHUNKS)) for p in range(1, SIDE * SIDE)} | {0: 0}
NEAR_AT = [0] + [max(Z_AT[c, d] for c in range(CHUNKS) for d in (h, CHIPS - h)) for h in range(1, CHIPS // 2 + 1)]


def kernel(
    v_hbm, tile_hbm, keep_hbm, thr_hbm, acc, scale_ref,
    row_panel, col_panel, loaded, tile_ref, keep_ref, thr_ref, colsum, stats, sums, psum,
    xy_send, xy_recv, z_send, z_recv, pair_send, pair_recv,
    small_send, small_recv, load_sem, hello,
):
    rows, cols = v_hbm.shape
    part = rows // CHUNKS
    order = rows * SIDE * SIDE
    me_row, me_col = lax.axis_index("row"), lax.axis_index("col")
    x, y = me_row // SIDE, me_row % SIDE
    z, core = me_col // CORES, me_col % CORES

    def xy_device(dx, dy):
        return {"row": (x + dx + SIDE) % SIDE * SIDE + (y + dy + SIDE) % SIDE}

    def z_device(dz, lane=0):
        return {"col": (z + dz + CHIPS) % CHIPS * CORES + (core if lane == 0 else 1 - core)}

    neighbours = [xy_device(*link) for link in LINKS] + [z_device(1), z_device(-1), z_device(0, 1)]
    barrier = pltpu.get_barrier_semaphore()
    for device in neighbours:
        pl.semaphore_signal(barrier, inc=1, device_id=device)

    def load(q):
        spot = pl.ds(q * part, part)
        return pltpu.make_async_copy(v_hbm.at[spot], loaded.at[spot], load_sem.at[q])

    masks = (
        pltpu.make_async_copy(tile_hbm, tile_ref, load_sem.at[CHUNKS]),
        pltpu.make_async_copy(keep_hbm, keep_ref, load_sem.at[CHUNKS + 1]),
        pltpu.make_async_copy(thr_hbm, thr_ref, load_sem.at[CHUNKS + 2]),
    )
    masks[0].start()
    for q in range(CHUNKS):
        load(q).start()
    masks[1].start()
    masks[2].start()

    masks[0].wait()
    stored = tile_ref[...].astype(jnp.float32)
    for q in range(CHUNKS):
        load(q).wait()
        for lo in range(q * part, (q + 1) * part, min(part, TB)):
            for b in range(cols // TB):
                r, c = slice(lo, lo + min(part, TB)), slice(b * TB, (b + 1) * TB)
                i = lo // TB
                factor = jnp.broadcast_to(stored[i : i + 1, b : b + 1], (min(part, TB), TB))
                tile = (loaded[r, c].astype(jnp.float32) * factor).astype(jnp.bfloat16)
                row_panel[0, r, c] = tile
                col_panel[r, c] = tile

    pl.semaphore_wait(barrier, len(neighbours))

    def xy_copy(c, place, n):
        to = shift(place, n)
        return pltpu.make_async_remote_copy(
            src_ref=col_panel.at[pl.ds(place * rows + c * part, part)],
            dst_ref=col_panel.at[pl.ds(to * rows + c * part, part)],
            send_sem=xy_send.at[n], recv_sem=xy_recv.at[to, c],
            device_id=neighbours[n],
        )

    def z_copy(c, hop, n):
        sign = 1 - 2 * n
        spot = pl.ds(c * part, part)
        to = sign * (hop + 1) % CHIPS
        return pltpu.make_async_remote_copy(
            src_ref=row_panel.at[sign * hop % CHIPS * CORES, spot],
            dst_ref=row_panel.at[to * CORES, spot],
            send_sem=z_send.at[n], recv_sem=z_recv.at[to, c],
            device_id=neighbours[4 + n],
        )

    def pair_copy(c, dz):
        spot = pl.ds(c * part, part)
        return pltpu.make_async_remote_copy(
            src_ref=row_panel.at[dz * CORES, spot], dst_ref=row_panel.at[dz * CORES + 1, spot],
            send_sem=pair_send.at[0], recv_sem=pair_recv.at[dz, c],
            device_id=neighbours[6],
        )

    def send(s):
        for n in range(4):
            if s < SLOTS:
                xy_copy(*ORDER[n][s], n).start()
            if n < 2 and s < Z_SLOTS:
                z_copy(*Z_ORDER[n][s], n).start()

    for s in range(AHEAD):
        send(s)
    for c in range(CHUNKS):
        pair_copy(c, 0).start()

    def greet(k):
        for device in neighbours:
            pl.semaphore_signal(hello.at[k], inc=1, device_id=device)
        pl.semaphore_wait(hello.at[k], len(neighbours))

    total = jnp.zeros((1, cols), jnp.float32)
    for lo in range(0, rows, TB):
        block = col_panel[lo : lo + TB].astype(jnp.float32)
        total += jnp.sum(block, axis=0, keepdims=True)
    colsum[0] = total
    for k in range(3):
        greet(k)

    def spread(buffer, k, count, device):
        def copy(d):
            return pltpu.make_async_remote_copy(
                src_ref=buffer.at[0], dst_ref=buffer.at[d],
                send_sem=small_send.at[k], recv_sem=small_recv.at[k], device_id=device(d),
            )

        everything = pltpu.make_async_remote_copy(
            src_ref=buffer.at[pl.ds(1, count - 1)], dst_ref=buffer.at[pl.ds(1, count - 1)],
            send_sem=small_send.at[k], recv_sem=small_recv.at[k], device_id=neighbours[6],
        )
        return [copy(d) for d in range(1, count)], everything

    def by_row(d):
        return xy_device(d // SIDE, d % SIDE)

    def by_col(d):
        return z_device(d // CORES, d % CORES)

    column_sums, column_sums_all = spread(colsum, 0, SIDE * SIDE, by_row)
    for copy in column_sums:
        copy.start()
    greet(3)
    acc[...] = jnp.zeros((rows, cols), jnp.float32)
    psum[...] = jnp.zeros((EXTRA, cols), jnp.float32)

    block_sums, block_sums_all = spread(stats, 1, CHIPS * CORES, by_col)

    def send_block_sums():
        column_sums_all.wait_recv()
        column_sums_all.wait_send()
        total = colsum[0]
        for i in range(1, SIDE * SIDE):
            total += colsum[i]
        stats[0] = total
        for copy in block_sums:
            copy.start()

    def take_block_sums():
        block_sums_all.wait_recv()
        block_sums_all.wait_send()
        line = lax.broadcasted_iota(jnp.int32, (EXTRA, cols), 0)

        @pl.loop(0, CHIPS * CORES)
        def _(i):
            rest, spot = stats[i], jnp.zeros((EXTRA, cols), jnp.float32)
            for k in range(3):
                term = rest.astype(jnp.bfloat16).astype(jnp.float32)
                rest = rest - term
                spot = jnp.where(line == k, jnp.broadcast_to(term, (EXTRA, cols)), spot)
            row_panel[i, rows:] = spot.astype(jnp.bfloat16)

    def inner(j):
        k = (x - j // SIDE + SIDE) % SIDE * SIDE + (y - j % SIDE + SIDE) % SIDE
        dz = (z - k // CORES + CHIPS) % CHIPS
        lane = (core + k) % CORES
        return dz, lane

    def have(j, step):
        dz, lane = inner(j)
        here = j == 0
        for p in range(1, SIDE * SIDE):
            if BLOCK_AT[p] <= step:
                here = here | (j == p)
        near = [-1, -1]
        for h in range(CHIPS // 2 + 1):
            for side in range(CORES):
                if NEAR_AT[h] + side <= step:
                    near[side] = h
        there = None
        for side in range(CORES):
            one = (lane == side) & ((dz <= near[side]) | (dz >= CHIPS - near[side]))
            there = one if there is None else there | one
        return here & there

    def compute(step, before):
        @pl.loop(0, SIDE * SIDE)
        def _(j):
            go = have(j, step) if step is not None else (j != LAST)
            if before is not None:
                go = go & jnp.logical_not(have(j, before))

            @pl.when(go)
            def _():
                dz, lane = inner(j)
                block = col_panel[pl.ds(pl.multiple_of(j * rows, rows), rows)]
                term = jnp.dot(row_panel[dz * CORES + lane], block, preferred_element_type=jnp.float32)
                acc[...] += term[:rows]
                psum[...] += term[rows:]

    def take_xy(s):
        for n in range(4):
            c, place = ORDER[n][s]
            xy_copy(c, place, n).wait_recv()

    def take_z(s):
        for n in range(2):
            if s < Z_SLOTS:
                c, hop = Z_ORDER[n][s]
                z_copy(c, hop, n).wait_recv()
                pair_copy(c, (1 - 2 * n) * (hop + 1) % CHIPS).start()

    def take_pair(s):
        if s == 0:
            for c in range(CHUNKS):
                pair_copy(c, 0).wait_recv()
        elif s <= Z_SLOTS:
            for n in range(2):
                c, hop = Z_ORDER[n][s - 1]
                pair_copy(c, (1 - 2 * n) * (hop + 1) % CHIPS).wait_recv()

    before = None
    for s in range(SLOTS):
        take_z(s)
        take_pair(s)
        if s < SLOTS - 1:
            take_xy(s)
            send(s + AHEAD)
        if s == 3:
            send_block_sums()
        if s == 6:
            take_block_sums()
        if s in POINTS:
            compute(s, before)
            before = s
    compute(None, before)

    masks[1].wait()
    masks[2].wait()
    kept = keep_ref[...].astype(jnp.float32)
    level = 0.125 * thr_ref[...].astype(jnp.float32)
    take_xy(SLOTS - 1)
    dz, lane = inner(LAST)
    slot = dz * CORES + lane
    block = col_panel[LAST * rows : (LAST + 1) * rows]
    lines = psum[...] + jnp.dot(row_panel[slot, rows:], block, preferred_element_type=jnp.float32)
    cut = level * ((lines[2:3] + lines[1:2] + lines[0:1]) / order)
    parts = [jnp.zeros((1, TB), jnp.float32) for _ in range(cols // TB)]
    for lo in range(0, rows, TB):
        term = jnp.dot(row_panel[slot, lo : lo + TB], block, preferred_element_type=jnp.float32)
        for b in range(cols // TB):
            r, c = slice(lo, lo + TB), slice(b * TB, (b + 1) * TB)
            keep = jnp.broadcast_to(kept[lo // TB : lo // TB + 1, b : b + 1], (TB, TB))
            pruned = jnp.maximum(acc[r, c] + term[:, c] - cut[:, c], 0.0) * keep
            acc[r, c] = pruned
            parts[b] += jnp.sum(pruned, axis=0, keepdims=True)
    sums[0] = jnp.concatenate(parts, axis=1)

    totals, totals_all = spread(sums, 2, SIDE * SIDE, by_row)
    for copy in totals:
        copy.start()

    for n in range(4):
        spot = col_panel.at[pl.ds(0, SLOTS * part)]
        pltpu.make_async_remote_copy(
            src_ref=spot, dst_ref=spot, send_sem=xy_send.at[n], recv_sem=xy_send.at[n], device_id=neighbours[n]
        ).wait_send()
    for n in range(2):
        spot = col_panel.at[pl.ds(0, Z_SLOTS * part)]
        pltpu.make_async_remote_copy(
            src_ref=spot, dst_ref=spot, send_sem=z_send.at[n], recv_sem=z_send.at[n], device_id=neighbours[4 + n]
        ).wait_send()
    spot = col_panel.at[pl.ds(0, CHIPS * rows)]
    pltpu.make_async_remote_copy(
        src_ref=spot, dst_ref=spot, send_sem=pair_send.at[0], recv_sem=pair_send.at[0], device_id=neighbours[6]
    ).wait_send()

    totals_all.wait_send()
    totals_all.wait_recv()
    total = sums[0]
    for i in range(1, SIDE * SIDE):
        total += sums[i]
    scale_ref[...] = 1.0 / jnp.maximum(total / order, 0.1)


def on_device(values, tile_mask, keep_mask, thr_index):
    rows, cols = values.shape
    dma, plain = pltpu.SemaphoreType.DMA, pltpu.SemaphoreType.REGULAR
    vmem, anywhere = pl.BlockSpec(memory_space=pltpu.VMEM), pl.BlockSpec(memory_space=pl.ANY)
    blocks = SIDE * SIDE
    pruned, scale = pl.pallas_call(
        kernel,
        out_shape=(pltpu.VMEM((rows, cols), jnp.float32), pltpu.VMEM((1, cols), jnp.float32)),
        in_specs=[anywhere] * 4,
        out_specs=(vmem, vmem),
        scratch_shapes=[
            pltpu.VMEM((CHIPS * CORES, rows + EXTRA, cols), jnp.bfloat16),
            pltpu.VMEM((blocks * rows, cols), jnp.bfloat16),
            pltpu.VMEM((rows, cols), jnp.bfloat16),
            pltpu.VMEM(tile_mask.shape, jnp.int32),
            pltpu.VMEM(keep_mask.shape, jnp.int32),
            pltpu.VMEM((1, cols), jnp.int32),
            pltpu.VMEM((blocks, 1, cols), jnp.float32),
            pltpu.VMEM((CHIPS * CORES, 1, cols), jnp.float32),
            pltpu.VMEM((blocks, 1, cols), jnp.float32),
            pltpu.VMEM((EXTRA, cols), jnp.float32),
            dma((4,)),
            dma((blocks, CHUNKS)),
            dma((2,)),
            dma((CHIPS, CHUNKS)),
            dma((1,)),
            dma((CHIPS, CHUNKS)),
            dma((3,)),
            dma((3,)),
            dma((CHUNKS + 3,)),
            plain((4,)),
        ],
        compiler_params=pltpu.CompilerParams(
            collective_id=0, has_side_effects=True,
            vmem_limit_bytes=63 * 2**20 - 4 * rows * cols + 2**19,
        ),
    )(values, tile_mask, keep_mask, thr_index.reshape(1, cols))
    return (pruned * scale).astype(jnp.bfloat16)


def solution(mesh):
    return jax.shard_map(
        on_device,
        mesh=mesh,
        in_specs=(P("row", "col"), P("row", "col"), P("row", "col"), P("col")),
        out_specs=P("row", "col"),
        check_vma=False,
    )
```

time: 121 us -> 61.2 us (0.51)
  the two profiles are of different devices: /device:TPU:8 before, /device:TPU:1 now
where the time goes in v1:
time: 61.2 us; the launch traced here: 61.1 us
  Pallas kernels  60.2 us (98%)
  other arithmetic  0.91 us (1%)
    pallas_call x1, Pallas kernels, on_device(): pl.pallas_call(kernel, out_shape=(pltpu.VMEM((rows, cols), jnp.float32),...  60.2 us

profile of v1, /device:TPU:1, one launch (start us, length us, event | category | flops | bytes accessed | tf_op | source)
XLA Modules:
  0.0 61.1 jit_solution(9223661246472748116)
XLA Ops:
  0.0 60.2 %shard_map.46 = (f32[512,512]{1,0:T(8,128)S(1)}, f32[1,512]{1,0:T(1,128)S(1)}) custom-call(bf16[512,512]{1,0:T(8,128)(2,1)} %v_hbm.1, s32[4,4]{1,0:T(4,128)} %tile_hbm.1, s32[4,4]{1,0:T(4,128)} %keep_hbm.1, s32[1,512]{1,0:T(1,128)} %bitcast.3), custom_call_target="tpu_custom_call" | custom-call | tf_op jit(solution)/shard_map/pallas_call | solution.py:343
  60.2 0.9 %multiply_convert_fusion = bf16[512,512]{1,0:T(8,128)(2,1)} fusion(f32[512,512]{1,0:T(8,128)S(1)} %get-tuple-element.7, f32[512]{0:T(512)S(1)} %bitcast.2), kind=kLoop, calls=%fused_computation | loop fusion | flops 524288 | bytes 1574912 | tf_op jit(solution)/shard_map/convert_element_type | solution.py:375

commit v2 on v1

v2 whole, which is shorter than its diff:
```python
import functools

import jax
import jax.numpy as jnp
from jax import lax
from jax.experimental import pallas as pl
from jax.experimental.pallas import tpu as pltpu
from jax.sharding import PartitionSpec as P

TB = 128
CORES = 2
SIDE = 4
CHIPS = 8
CHUNKS = 4
LAST = 10
EXTRA = 16
LINKS = ((1, 0), (-1, 0), (0, 1), (0, -1))

ORDER = (
    ((0, 0), (1, 0), (2, 0), (3, 0), (0, 4), (2, 3), (3, 3), (2, 4), (2, 1), (3, 1), (2, 2), (3, 2), (2, 5), (2, 7), (2, 6)),
    ((1, 0), (0, 0), (3, 0), (2, 0), (1, 12), (3, 1), (2, 1), (3, 12), (3, 3), (2, 3), (3, 2), (2, 2), (3, 13), (3, 15), (3, 14)),
    ((2, 0), (3, 0), (0, 0), (1, 0), (2, 1), (0, 12), (1, 12), (0, 4), (0, 1), (1, 4), (0, 8), (0, 13), (1, 8), (0, 5), (0, 9)),
    ((3, 0), (2, 0), (1, 0), (0, 0), (3, 3), (1, 4), (0, 4), (1, 12), (1, 3), (0, 12), (1, 8), (1, 15), (1, 7), (0, 8), (1, 11)),
)
SLOTS = len(ORDER[0])
Z_ORDER = (
    tuple((c, hop) for hop in range(3) for c in (0, 1, 2, 3)) + ((0, 3), (1, 3)),
    tuple((c, hop) for hop in range(3) for c in (2, 3, 0, 1)) + ((2, 3), (3, 3)),
)
Z_SLOTS = len(Z_ORDER[0])
AHEAD = 4
POINTS = (3, 5, 7, 9, 11, 12, 13)
SUMMED = (11, 12)


def shift(place, link):
    dx, dy = LINKS[link]
    return (place // SIDE + dx) % SIDE * SIDE + (place % SIDE + dy) % SIDE


def arrivals():
    xy = {(c, shift(p, n)): s for n in range(4) for s, (c, p) in enumerate(ORDER[n])}
    z = {}
    for n, sign in ((0, 1), (1, -1)):
        for s, (c, hop) in enumerate(Z_ORDER[n]):
            z[c, sign * (hop + 1) % CHIPS] = s
    return xy, z


XY_AT, Z_AT = arrivals()
BLOCK_AT = {p: max(XY_AT[c, p] for c in range(CHUNKS)) for p in range(1, SIDE * SIDE)} | {0: 0}
Z_TAKEN = {at: at + 1 for at in range(Z_SLOTS - 2)}
NEAR_AT = [(-1, 0)] + [
    (due, due + 1) for due in (
        max(Z_TAKEN[Z_AT[c, d]] for c in range(CHUNKS) for d in (h, CHIPS - h)) for h in range(1, CHIPS // 2)
    )
] + [(SLOTS - 1.4, SLOTS - 1.2)]
NEAR_AT[-2] = (NEAR_AT[-2][0], NEAR_AT[-2][0] + 0.5)


def kernel(
    v_hbm, tile_hbm, keep_hbm, thr_hbm, acc, scale_ref,
    row_panel, col_panel, loaded, tile_ref, keep_ref, thr_ref, colsum, stats, sums, psum,
    bulk_send, xy_recv, z_recv, pair_recv,
    small_send, small_recv, load_sem, ready, hello,
):
    rows, cols = v_hbm.shape
    part = rows // CHUNKS
    order = rows * SIDE * SIDE
    me_row, me_col = lax.axis_index("row"), lax.axis_index("col")
    x, y = me_row // SIDE, me_row % SIDE
    z, core = me_col // CORES, me_col % CORES

    def xy_device(dx, dy):
        return {"row": (x + dx + SIDE) % SIDE * SIDE + (y + dy + SIDE) % SIDE}

    def z_device(dz, lane=0):
        return {"col": (z + dz + CHIPS) % CHIPS * CORES + (core if lane == 0 else 1 - core)}

    neighbours = [xy_device(*link) for link in LINKS] + [z_device(1), z_device(-1), z_device(0, 1)]
    later = [x < SIDE - 1, x == 0, y < SIDE - 1, y == 0, z < CHIPS - 1, z == 0, core == 1]
    barrier = pltpu.get_barrier_semaphore()
    earlier = 0
    for n, device in enumerate(neighbours):
        earlier = earlier + 1 - later[n].astype(jnp.int32)

        @pl.when(later[n])
        def _():
            pl.semaphore_signal(barrier, inc=1, device_id=device)

    def load(q):
        spot = pl.ds(q * part, part)
        return pltpu.make_async_copy(v_hbm.at[spot], loaded.at[spot], load_sem.at[q])

    masks = (
        pltpu.make_async_copy(tile_hbm, tile_ref, load_sem.at[CHUNKS]),
        pltpu.make_async_copy(keep_hbm, keep_ref, load_sem.at[CHUNKS + 1]),
        pltpu.make_async_copy(thr_hbm, thr_ref, load_sem.at[CHUNKS + 2]),
    )
    masks[0].start()
    for q in range(CHUNKS):
        load(q).start()
    masks[1].start()
    masks[2].start()

    def xy_copy(c, place, n):
        to = shift(place, n)
        return pltpu.make_async_remote_copy(
            src_ref=col_panel.at[pl.ds(place * rows + c * part, part)],
            dst_ref=col_panel.at[pl.ds(to * rows + c * part, part)],
            send_sem=bulk_send.at[0], recv_sem=xy_recv.at[XY_AT[c, to]],
            device_id=neighbours[n],
        )

    def z_copy(c, hop, n):
        sign = 1 - 2 * n
        spot = pl.ds(c * part, part)
        to = sign * (hop + 1) % CHIPS
        return pltpu.make_async_remote_copy(
            src_ref=row_panel.at[sign * hop % CHIPS * CORES, spot],
            dst_ref=row_panel.at[to * CORES, spot],
            send_sem=bulk_send.at[1], recv_sem=z_recv.at[Z_AT[c, to]],
            device_id=neighbours[4 + n],
        )

    def pair_copy(c, dz):
        spot = pl.ds(c * part, part)
        return pltpu.make_async_remote_copy(
            src_ref=row_panel.at[dz * CORES, spot], dst_ref=row_panel.at[dz * CORES + 1, spot],
            send_sem=bulk_send.at[1], recv_sem=pair_recv.at[min(dz, CHIPS - dz)],
            device_id=neighbours[6],
        )

    def send(n, s):
        if n < 4 and s < SLOTS:
            xy_copy(*ORDER[n][s], n).start()
        elif n == 6 and s < CHUNKS:
            pair_copy(s, 0).start()
        elif n in (4, 5) and s < Z_SLOTS:
            z_copy(*Z_ORDER[n - 4][s], n - 4).start()

    @pl.when(earlier > 0)
    def _():
        pl.semaphore_wait(barrier, earlier)

    for n, device in enumerate(neighbours):
        @pl.when(jnp.logical_not(later[n]))
        def _():
            pl.semaphore_signal(ready.at[n ^ 1 if n < 6 else n], inc=1, device_id=device)

    masks[0].wait()
    stored = tile_ref[...].astype(jnp.float32)
    for q in range(CHUNKS):
        load(q).wait()
        for lo in range(q * part, (q + 1) * part, min(part, TB)):
            for b in range(cols // TB):
                r, c = slice(lo, lo + min(part, TB)), slice(b * TB, (b + 1) * TB)
                i = lo // TB
                factor = jnp.broadcast_to(stored[i : i + 1, b : b + 1], (min(part, TB), TB))
                tile = (loaded[r, c].astype(jnp.float32) * factor).astype(jnp.bfloat16)
                row_panel[0, r, c] = tile
                col_panel[r, c] = tile

    def when_not(n, do):
        @pl.when(jnp.logical_not(later[n]))
        def _():
            do()

    for s in range(AHEAD):
        for n in range(7):
            when_not(n, lambda: send(n, s))
    for n in (6, 0, 2, 4, 1, 3, 5):
        @pl.when(later[n])
        def _():
            with jax.named_scope(f"open{n}"):
                pl.semaphore_wait(ready.at[n], 1)
            for s in range(AHEAD):
                send(n, s)

    def greet(k, over):
        for device in neighbours[4 * over : 4 + 3 * over]:
            pl.semaphore_signal(hello.at[2 * over + k % 2], inc=1, device_id=device)

    def greeted(k, over):
        pl.semaphore_wait(hello.at[2 * over + k % 2], 4 - over)

    greet(0, 0)
    greet(0, 1)

    def spread(buffer, k, count, device):
        def copy(d):
            return pltpu.make_async_remote_copy(
                src_ref=buffer.at[0], dst_ref=buffer.at[d],
                send_sem=small_send.at[0], recv_sem=small_recv.at[k], device_id=device(d),
            )

        everything = pltpu.make_async_remote_copy(
            src_ref=buffer.at[pl.ds(1, count - 1)], dst_ref=buffer.at[pl.ds(1, count - 1)],
            send_sem=small_send.at[0], recv_sem=small_recv.at[k], device_id=neighbours[6],
        )
        return [copy(d) for d in range(1, count)], everything

    def by_row(d):
        return xy_device(d // SIDE, d % SIDE)

    def by_col(d):
        return z_device(d)

    column_sums, column_sums_all = spread(colsum, 0, SIDE * SIDE, by_row)

    def sum_columns():
        total = jnp.zeros((1, cols), jnp.float32)
        for lo in range(0, rows, TB):
            block = col_panel[lo : lo + TB].astype(jnp.float32)
            total += jnp.sum(block, axis=0, keepdims=True)
        colsum[0] = total

    block_sums, block_sums_all = spread(stats, 1, CHIPS, by_col)

    def send_block_sums():
        column_sums_all.wait_recv()
        column_sums_all.wait_send()
        total = colsum[0]
        for i in range(1, SIDE * SIDE):
            total += colsum[i]
        stats[0] = total
        for copy in block_sums:
            copy.start()

    pair_sums = pltpu.make_async_remote_copy(
        src_ref=stats.at[pl.ds(0, CHIPS)], dst_ref=stats.at[pl.ds(CHIPS, CHIPS)],
        send_sem=small_send.at[0], recv_sem=small_recv.at[3], device_id=neighbours[6],
    )

    def pass_block_sums():
        block_sums_all.wait_recv()
        block_sums_all.wait_send()
        pair_sums.start()

    def take_block_sums():
        pair_sums.wait()
        line = lax.broadcasted_iota(jnp.int32, (EXTRA, cols), 0)

        @pl.loop(0, CHIPS * CORES)
        def _(i):
            rest, spot = stats[i], jnp.zeros((EXTRA, cols), jnp.float32)
            for k in range(3):
                term = rest.astype(jnp.bfloat16).astype(jnp.float32)
                rest = rest - term
                spot = jnp.where(line == k, jnp.broadcast_to(term, (EXTRA, cols)), spot)
            row_panel[i % CHIPS * CORES + i // CHIPS, rows:] = spot.astype(jnp.bfloat16)

    def inner(j):
        k = (x - j // SIDE + SIDE) % SIDE * SIDE + (y - j % SIDE + SIDE) % SIDE
        dz = (z - k // CORES + CHIPS) % CHIPS
        lane = (core + k) % CORES
        return dz, lane

    def near(dz, lane, step):
        there = None
        for side in range(CORES):
            reach = max([h for h in range(CHIPS // 2 + 1) if NEAR_AT[h][side] <= step], default=-1)
            one = (lane == side) & ((dz <= reach) | (dz >= CHIPS - reach))
            there = one if there is None else there | one
        return there

    def pick(i, values):
        found = values[0]
        for k, value in enumerate(values[1:], 1):
            found = found + (i == k).astype(jnp.int32) * (value - values[0])
        return found

    def multiply(j):
        dz, lane = inner(j)
        block = col_panel[pl.ds(pl.multiple_of(j * rows, rows), rows)]
        acc[...] += jnp.dot(
            row_panel[dz * CORES + lane, :rows], block, preferred_element_type=jnp.float32
        )

    def compute(step, before):
        fresh = [p for p in range(SIDE * SIDE) if p != LAST and before < BLOCK_AT[p] <= step]
        assert before < step
        if fresh:
            @pl.loop(0, len(fresh))
            def _(i):
                j = pick(i, fresh)

                @pl.when(near(*inner(j), step))
                def _():
                    multiply(j)

        old = [p for p in range(SIDE * SIDE) if p != LAST and BLOCK_AT[p] <= before]
        came = [
            (dz, side) for side in range(CORES) for h in range(CHIPS // 2 + 1)
            for dz in sorted({h, (CHIPS - h) % CHIPS}) if before < NEAR_AT[h][side] <= step
        ]
        if old and came:
            @pl.loop(0, len(came))
            def _(i):
                dz = pick(i, [c[0] for c in came])
                side = pick(i, [c[1] for c in came])
                k = (z - dz + CHIPS) % CHIPS * CORES + (core + side) % CORES
                j = (x - k // SIDE + SIDE) % SIDE * SIDE + (y - k % SIDE + SIDE) % SIDE
                met = j == old[0]
                for p in old[1:]:
                    met = met | (j == p)

                @pl.when(met)
                def _():
                    multiply(j)

    def add_sums(step, before):
        fresh = [p for p in range(SIDE * SIDE) if p != LAST and before < BLOCK_AT[p] <= step]

        @pl.loop(0, len(fresh))
        def _(i):
            j = pick(i, fresh)
            dz, lane = inner(j)
            block = col_panel[pl.ds(pl.multiple_of(j * rows, rows), rows)]
            psum[...] += jnp.dot(
                row_panel[dz * CORES + lane, rows:], block, preferred_element_type=jnp.float32
            )

    def await_rows(count, sem):
        spot = col_panel.at[pl.ds(0, count)]
        pltpu.make_async_remote_copy(
            src_ref=spot, dst_ref=spot, send_sem=bulk_send.at[0], recv_sem=sem, device_id=neighbours[0]
        ).wait_recv()

    def take_xy(s):
        await_rows(4 * part, xy_recv.at[s])

    def take_z(s):
        if s < Z_SLOTS:
            await_rows(2 * part, z_recv.at[s])
            for (c, dz), at in sorted(Z_AT.items()):
                if at == s:
                    pair_copy(c, dz).start()

    def take_pair(h):
        await_rows(len({h, -h % CHIPS}) * rows, pair_recv.at[h])

    before, summed = -1, -1
    for s in range(SLOTS - 1):
        if s < SLOTS - 1:
            with jax.named_scope(f"xy{s}"):
                take_xy(s)
            for n in range(4):
                send(n, s + AHEAD)
        for at in range(Z_SLOTS):
            if Z_TAKEN.get(at) == s:
                with jax.named_scope(f"z{at}"):
                    take_z(at)
        for n in (4, 5):
            if s > 0:
                send(n, s + AHEAD - 1)
        for h in range(CHIPS // 2):
            if s == NEAR_AT[h][1]:
                with jax.named_scope(f"pair{h}"):
                    take_pair(h)
        if s == Z_SLOTS - 1:
            @pl.when(z != 0)
            def _():
                take_z(s - 1)
                take_z(s)
        with jax.named_scope(f"sums{s}"):
            if s == 0:
                sum_columns()
                acc[...] = jnp.zeros((rows, cols), jnp.float32)
                psum[...] = jnp.zeros((EXTRA, cols), jnp.float32)
            if s < 3:
                greeted(s, 0)
                if s < 2:
                    greet(s + 1, 0)
            if s in (2, 4, 6):
                greeted(s // 2 - 1, 1)
                if s < 6:
                    greet(s // 2, 1)
            if s == 2:
                for copy in column_sums:
                    copy.start()
            if s == 6:
                send_block_sums()
            if s == 9:
                pass_block_sums()
            if s == 11:
                take_block_sums()
        if s in POINTS:
            with jax.named_scope(f"multiply{s}"):
                compute(s, before)
            before = s
        if s in SUMMED:
            with jax.named_scope(f"add{s}"):
                add_sums(s, summed)
            summed = s
        if s == Z_SLOTS - 2:
            with jax.named_scope("pair3"):
                take_pair(CHIPS // 2 - 1)
            with jax.named_scope("multiply3b"):
                compute(NEAR_AT[-2][1], before)
            before = NEAR_AT[-2][1]

    @pl.when(z == 0)
    def _():
        with jax.named_scope("zlast"):
            take_z(Z_SLOTS - 2)
            take_z(Z_SLOTS - 1)
    with jax.named_scope("multiplyA"):
        compute(NEAR_AT[-1][0], before)
    with jax.named_scope("addA"):
        add_sums(SLOTS - 2, summed)
    with jax.named_scope("pairlast"):
        take_pair(CHIPS // 2)
    with jax.named_scope("multiplyB"):
        compute(NEAR_AT[-1][1], NEAR_AT[-1][0])

    masks[1].wait()
    masks[2].wait()
    kept = keep_ref[...].astype(jnp.float32)
    level = 0.125 * thr_ref[...].astype(jnp.float32)
    with jax.named_scope("xy"):
        take_xy(SLOTS - 1)
    dz, lane = inner(LAST)
    slot = dz * CORES + lane
    block = col_panel[LAST * rows : (LAST + 1) * rows]
    lines = psum[...] + jnp.dot(row_panel[slot, rows:], block, preferred_element_type=jnp.float32)
    cut = level * ((lines[2:3] + lines[1:2] + lines[0:1]) / order)
    parts = [jnp.zeros((1, TB), jnp.float32) for _ in range(cols // TB)]
    for lo in range(0, rows, TB):
        term = jnp.dot(row_panel[slot, lo : lo + TB], block, preferred_element_type=jnp.float32)
        for b in range(cols // TB):
            r, c = slice(lo, lo + TB), slice(b * TB, (b + 1) * TB)
            keep = jnp.broadcast_to(kept[lo // TB : lo // TB + 1, b : b + 1], (TB, TB))
            pruned = jnp.maximum(acc[r, c] + term[:, c] - cut[:, c], 0.0) * keep
            acc[r, c] = pruned
            parts[b] += jnp.sum(pruned, axis=0, keepdims=True)
    sums[0] = jnp.concatenate(parts, axis=1)

    totals, totals_all = spread(sums, 2, SIDE * SIDE, by_row)
    for copy in totals:
        copy.start()

    for k, count in enumerate((4 * SLOTS * part, 2 * Z_SLOTS * part + CHIPS * rows)):
        spot = col_panel.at[pl.ds(0, count)]
        pltpu.make_async_remote_copy(
            src_ref=spot, dst_ref=spot, send_sem=bulk_send.at[k], recv_sem=bulk_send.at[k],
            device_id=neighbours[0],
        ).wait_send()

    with jax.named_scope("totals"):
        totals_all.wait_send()
        totals_all.wait_recv()
    total = sums[0]
    for i in range(1, SIDE * SIDE):
        total += sums[i]
    scale_ref[...] = 1.0 / jnp.maximum(total / order, 0.1)


def on_device(values, tile_mask, keep_mask, thr_index):
    rows, cols = values.shape
    dma, plain = pltpu.SemaphoreType.DMA, pltpu.SemaphoreType.REGULAR
    vmem, anywhere = pl.BlockSpec(memory_space=pltpu.VMEM), pl.BlockSpec(memory_space=pl.ANY)
    blocks = SIDE * SIDE
    pruned, scale = pl.pallas_call(
        kernel,
        out_shape=(pltpu.VMEM((rows, cols), jnp.float32), pltpu.VMEM((1, cols), jnp.float32)),
        in_specs=[anywhere] * 4,
        out_specs=(vmem, vmem),
        scratch_shapes=[
            pltpu.VMEM((CHIPS * CORES, rows + EXTRA, cols), jnp.bfloat16),
            pltpu.VMEM((blocks * rows, cols), jnp.bfloat16),
            pltpu.VMEM((rows, cols), jnp.bfloat16),
            pltpu.VMEM(tile_mask.shape, jnp.int32),
            pltpu.VMEM(keep_mask.shape, jnp.int32),
            pltpu.VMEM((1, cols), jnp.int32),
            pltpu.VMEM((blocks, 1, cols), jnp.float32),
            pltpu.VMEM((CHIPS * CORES, 1, cols), jnp.float32),
            pltpu.VMEM((blocks, 1, cols), jnp.float32),
            pltpu.VMEM((EXTRA, cols), jnp.float32),
            dma((2,)),
            dma((SLOTS,)),
            dma((Z_SLOTS,)),
            dma((CHIPS // 2 + 1,)),
            dma((1,)),
            dma((4,)),
            dma((CHUNKS + 3,)),
            plain((7,)),
            plain((4,)),
        ],
        compiler_params=pltpu.CompilerParams(
            collective_id=0, has_side_effects=True,
            vmem_limit_bytes=63 * 2**20 - 4 * rows * cols + 2**19,
        ),
    )(values, tile_mask, keep_mask, thr_index.reshape(1, cols))
    return (pruned * scale).astype(jnp.bfloat16)


def solution(mesh):
    return jax.shard_map(
        on_device,
        mesh=mesh,
        in_specs=(P("row", "col"), P("row", "col"), P("row", "col"), P("col")),
        out_specs=P("row", "col"),
        check_vma=False,
    )
```

time: 61.2 us -> 59.5 us (0.972)
  Pallas kernels: 60.2 us -> 58.5 us
    pallas_call x1, Pallas kernels: 60.2 us -> 58.5 us  [on_device(): pl.pallas_call(kernel, out_shape=(pltpu.VMEM((rows, cols), jnp.float32),...]
where the time goes in v2:
time: 59.5 us; the launch traced here: 59.4 us
  Pallas kernels  58.5 us (98%)
  other arithmetic  0.91 us (2%)
    pallas_call x1, Pallas kernels, on_device(): pl.pallas_call(kernel, out_shape=(pltpu.VMEM((rows, cols), jnp.float32),...  58.5 us

profile of v2, /device:TPU:1, one launch (start us, length us, event | category | flops | bytes accessed | tf_op | source)
XLA Modules:
  0.0 59.4 jit_solution(3911569300882071950)
XLA Ops:
  0.0 58.5 %shard_map.46 = (f32[512,512]{1,0:T(8,128)S(1)}, f32[1,512]{1,0:T(1,128)S(1)}) custom-call(bf16[512,512]{1,0:T(8,128)(2,1)} %v_hbm.1, s32[4,4]{1,0:T(4,128)} %tile_hbm.1, s32[4,4]{1,0:T(4,128)} %keep_hbm.1, s32[1,512]{1,0:T(1,128)} %bitcast.3), custom_call_target="tpu_custom_call" | custom-call | tf_op jit(solution)/shard_map/pallas_call | solution.py:464
  58.5 0.9 %multiply_convert_fusion = bf16[512,512]{1,0:T(8,128)(2,1)} fusion(f32[512,512]{1,0:T(8,128)S(1)} %get-tuple-element.7, f32[512]{0:T(512)S(1)} %bitcast.2), kind=kLoop, calls=%fused_computation | loop fusion | flops 524288 | bytes 1574912 | tf_op jit(solution)/shard_map/convert_element_type | solution.py:495

commit v3 on v2

--- a/solution.py
+++ b/solution.py
@@ -24,13 +24,14 @@
 )
 SLOTS = len(ORDER[0])
 Z_ORDER = (
-    tuple((c, hop) for hop in range(3) for c in (0, 1, 2, 3)) + ((0, 3), (1, 3)),
+    tuple((c, hop) for hop in range(3) for c in (1, 0, 2, 3)) + ((1, 3), (0, 3)),
     tuple((c, hop) for hop in range(3) for c in (2, 3, 0, 1)) + ((2, 3), (3, 3)),
 )
+DETOUR = (0, 3)
 Z_SLOTS = len(Z_ORDER[0])
 AHEAD = 4
 POINTS = (3, 5, 7, 9, 11, 12, 13)
-SUMMED = (11, 12)
+SUMMED = 10
 
 
 def shift(place, link):
@@ -49,20 +50,15 @@
 
 XY_AT, Z_AT = arrivals()
 BLOCK_AT = {p: max(XY_AT[c, p] for c in range(CHUNKS)) for p in range(1, SIDE * SIDE)} | {0: 0}
-Z_TAKEN = {at: at + 1 for at in range(Z_SLOTS - 2)}
-NEAR_AT = [(-1, 0)] + [
-    (due, due + 1) for due in (
-        max(Z_TAKEN[Z_AT[c, d]] for c in range(CHUNKS) for d in (h, CHIPS - h)) for h in range(1, CHIPS // 2)
-    )
-] + [(SLOTS - 1.4, SLOTS - 1.2)]
-NEAR_AT[-2] = (NEAR_AT[-2][0], NEAR_AT[-2][0] + 0.5)
+Z_LAG = 10
+NEAR_AT = [(-1, 0), (4, 5), (8, 9), (11.5, 12.5), (13.6, 13.8)]
 
 
 def kernel(
     v_hbm, tile_hbm, keep_hbm, thr_hbm, acc, scale_ref,
     row_panel, col_panel, loaded, tile_ref, keep_ref, thr_ref, colsum, stats, sums, psum,
     bulk_send, xy_recv, z_recv, pair_recv,
-    small_send, small_recv, load_sem, ready, hello,
+    detour_send, small_send, small_recv, load_sem, ready, hello,
 ):
     rows, cols = v_hbm.shape
     part = rows // CHUNKS
@@ -112,14 +108,14 @@
             device_id=neighbours[n],
         )
 
-    def z_copy(c, hop, n):
+    def z_copy(c, hop, n, sent=None):
         sign = 1 - 2 * n
         spot = pl.ds(c * part, part)
         to = sign * (hop + 1) % CHIPS
         return pltpu.make_async_remote_copy(
             src_ref=row_panel.at[sign * hop % CHIPS * CORES, spot],
             dst_ref=row_panel.at[to * CORES, spot],
-            send_sem=bulk_send.at[1], recv_sem=z_recv.at[Z_AT[c, to]],
+            send_sem=bulk_send.at[1] if sent is None else sent, recv_sem=z_recv.at[Z_AT[c, to]],
             device_id=neighbours[4 + n],
         )
 
@@ -137,7 +133,12 @@
         elif n == 6 and s < CHUNKS:
             pair_copy(s, 0).start()
         elif n in (4, 5) and s < Z_SLOTS:
-            z_copy(*Z_ORDER[n - 4][s], n - 4).start()
+            if n == 4 and Z_ORDER[0][s] == DETOUR:
+                @pl.when(z != CHIPS - 1)
+                def _():
+                    z_copy(*DETOUR, 0, detour_send.at[0]).start()
+            else:
+                z_copy(*Z_ORDER[n - 4][s], n - 4).start()
 
     @pl.when(earlier > 0)
     def _():
@@ -166,15 +167,18 @@
         def _():
             do()
 
-    for s in range(AHEAD):
-        for n in range(7):
+    for s in range(AHEAD - 1):
+        for n in range(6):
             when_not(n, lambda: send(n, s))
     for n in (6, 0, 2, 4, 1, 3, 5):
+        if n == 6:
+            when_not(n, lambda: [send(n, s) for s in range(CHUNKS)])
+
         @pl.when(later[n])
         def _():
             with jax.named_scope(f"open{n}"):
                 pl.semaphore_wait(ready.at[n], 1)
-            for s in range(AHEAD):
+            for s in range(CHUNKS if n == 6 else AHEAD - 1):
                 send(n, s)
 
     def greet(k, over):
@@ -208,12 +212,22 @@
 
     column_sums, column_sums_all = spread(colsum, 0, SIDE * SIDE, by_row)
 
-    def sum_columns():
-        total = jnp.zeros((1, cols), jnp.float32)
-        for lo in range(0, rows, TB):
-            block = col_panel[lo : lo + TB].astype(jnp.float32)
-            total += jnp.sum(block, axis=0, keepdims=True)
-        colsum[0] = total
+    total = jnp.zeros((1, cols), jnp.float32)
+    for lo in range(0, rows, TB):
+        block = col_panel[lo : lo + TB].astype(jnp.float32)
+        total += jnp.sum(block, axis=0, keepdims=True)
+    colsum[0] = total
+    acc[...] = jnp.zeros((rows, cols), jnp.float32)
+    psum[...] = jnp.zeros((EXTRA, cols), jnp.float32)
+    with jax.named_scope("greet"):
+        for k in range(3):
+            greeted(k, 0)
+            if k < 2:
+                greet(k + 1, 0)
+    for copy in column_sums:
+        copy.start()
+    for n in range(6):
+        send(n, AHEAD - 1)
 
     block_sums, block_sums_all = spread(stats, 1, CHIPS, by_col)
 
@@ -270,12 +284,17 @@
             found = found + (i == k).astype(jnp.int32) * (value - values[0])
         return found
 
-    def multiply(j):
+    def multiply(j, summed):
         dz, lane = inner(j)
         block = col_panel[pl.ds(pl.multiple_of(j * rows, rows), rows)]
-        acc[...] += jnp.dot(
-            row_panel[dz * CORES + lane, :rows], block, preferred_element_type=jnp.float32
-        )
+        if summed:
+            term = jnp.dot(row_panel[dz * CORES + lane], block, preferred_element_type=jnp.float32)
+            acc[...] += term[:rows]
+            psum[...] += term[rows:]
+        else:
+            acc[...] += jnp.dot(
+                row_panel[dz * CORES + lane, :rows], block, preferred_element_type=jnp.float32
+            )
 
     def compute(step, before):
         fresh = [p for p in range(SIDE * SIDE) if p != LAST and before < BLOCK_AT[p] <= step]
@@ -287,7 +306,7 @@
 
                 @pl.when(near(*inner(j), step))
                 def _():
-                    multiply(j)
+                    multiply(j, step > SUMMED)
 
         old = [p for p in range(SIDE * SIDE) if p != LAST and BLOCK_AT[p] <= before]
         came = [
@@ -307,19 +326,22 @@
 
                 @pl.when(met)
                 def _():
-                    multiply(j)
-
-    def add_sums(step, before):
-        fresh = [p for p in range(SIDE * SIDE) if p != LAST and before < BLOCK_AT[p] <= step]
+                    multiply(j, step > SUMMED)
+
+    def add_sums(step):
+        fresh = [p for p in range(SIDE * SIDE) if BLOCK_AT[p] <= step]
 
         @pl.loop(0, len(fresh))
         def _(i):
             j = pick(i, fresh)
             dz, lane = inner(j)
-            block = col_panel[pl.ds(pl.multiple_of(j * rows, rows), rows)]
-            psum[...] += jnp.dot(
-                row_panel[dz * CORES + lane, rows:], block, preferred_element_type=jnp.float32
-            )
+
+            @pl.when(near(dz, lane, step))
+            def _():
+                block = col_panel[pl.ds(pl.multiple_of(j * rows, rows), rows)]
+                psum[...] += jnp.dot(
+                    row_panel[dz * CORES + lane, rows:], block, preferred_element_type=jnp.float32
+                )
 
     def await_rows(count, sem):
         spot = col_panel.at[pl.ds(0, count)]
@@ -340,17 +362,16 @@
     def take_pair(h):
         await_rows(len({h, -h % CHIPS}) * rows, pair_recv.at[h])
 
-    before, summed = -1, -1
+    before = -1
     for s in range(SLOTS - 1):
         if s < SLOTS - 1:
             with jax.named_scope(f"xy{s}"):
                 take_xy(s)
             for n in range(4):
                 send(n, s + AHEAD)
-        for at in range(Z_SLOTS):
-            if Z_TAKEN.get(at) == s:
-                with jax.named_scope(f"z{at}"):
-                    take_z(at)
+        if 0 < s <= Z_LAG:
+            with jax.named_scope(f"z{s - 1}"):
+                take_z(s - 1)
         for n in (4, 5):
             if s > 0:
                 send(n, s + AHEAD - 1)
@@ -359,56 +380,40 @@
                 with jax.named_scope(f"pair{h}"):
                     take_pair(h)
         if s == Z_SLOTS - 1:
-            @pl.when(z != 0)
-            def _():
-                take_z(s - 1)
+            with jax.named_scope(f"z{s}"):
                 take_z(s)
         with jax.named_scope(f"sums{s}"):
-            if s == 0:
-                sum_columns()
-                acc[...] = jnp.zeros((rows, cols), jnp.float32)
-                psum[...] = jnp.zeros((EXTRA, cols), jnp.float32)
             if s < 3:
-                greeted(s, 0)
+                greeted(s, 1)
                 if s < 2:
-                    greet(s + 1, 0)
-            if s in (2, 4, 6):
-                greeted(s // 2 - 1, 1)
-                if s < 6:
-                    greet(s // 2, 1)
-            if s == 2:
-                for copy in column_sums:
-                    copy.start()
-            if s == 6:
+                    greet(s + 1, 1)
+            if s == 3:
                 send_block_sums()
-            if s == 9:
+            if s == SUMMED - 1:
                 pass_block_sums()
-            if s == 11:
+            if s == SUMMED:
                 take_block_sums()
+                add_sums(before)
         if s in POINTS:
             with jax.named_scope(f"multiply{s}"):
                 compute(s, before)
             before = s
-        if s in SUMMED:
-            with jax.named_scope(f"add{s}"):
-                add_sums(s, summed)
-            summed = s
         if s == Z_SLOTS - 2:
             with jax.named_scope("pair3"):
                 take_pair(CHIPS // 2 - 1)
             with jax.named_scope("multiply3b"):
                 compute(NEAR_AT[-2][1], before)
             before = NEAR_AT[-2][1]
-
-    @pl.when(z == 0)
-    def _():
-        with jax.named_scope("zlast"):
-            take_z(Z_SLOTS - 2)
-            take_z(Z_SLOTS - 1)
+        if Z_LAG <= s < Z_SLOTS - 1:
+            with jax.named_scope(f"z{s}"):
+                take_z(s)
+            if s == Z_AT[DETOUR[0], CHIPS - DETOUR[1]]:
+                @pl.when(z == 1)
+                def _():
+                    z_copy(*DETOUR, 1, detour_send.at[1]).start()
+
     with jax.named_scope("multiplyA"):
         compute(NEAR_AT[-1][0], before)
-    with jax.named_scope("addA"):
-        add_sums(SLOTS - 2, summed)
     with jax.named_scope("pairlast"):
         take_pair(CHIPS // 2)
     with jax.named_scope("multiplyB"):
@@ -440,12 +445,17 @@
     for copy in totals:
         copy.start()
 
-    for k, count in enumerate((4 * SLOTS * part, 2 * Z_SLOTS * part + CHIPS * rows)):
+    for k, count in enumerate((4 * SLOTS * part, (2 * Z_SLOTS - 1) * part + CHIPS * rows)):
         spot = col_panel.at[pl.ds(0, count)]
         pltpu.make_async_remote_copy(
             src_ref=spot, dst_ref=spot, send_sem=bulk_send.at[k], recv_sem=bulk_send.at[k],
             device_id=neighbours[0],
         ).wait_send()
+
+    for n, sends in ((0, z != CHIPS - 1), (1, z == 1)):
+        @pl.when(sends)
+        def _():
+            z_copy(*DETOUR, n, detour_send.at[n]).wait_send()
 
     with jax.named_scope("totals"):
         totals_all.wait_send()
@@ -481,6 +491,7 @@
             dma((SLOTS,)),
             dma((Z_SLOTS,)),
             dma((CHIPS // 2 + 1,)),
+            dma((2,)),
             dma((1,)),
             dma((4,)),
             dma((CHUNKS + 3,)),

time: 59.5 us -> 58.2 us (0.978)
  Pallas kernels: 58.5 us -> 57.2 us
    pallas_call x1, Pallas kernels: 58.5 us -> 57.2 us  [on_device(): pl.pallas_call(kernel, out_shape=(pltpu.VMEM((rows, cols), jnp.float32),...]
where the time goes in v3:
time: 58.2 us; the launch traced here: 58.1 us
  Pallas kernels  57.2 us (98%)
  other arithmetic  0.91 us (2%)
    pallas_call x1, Pallas kernels, on_device(): pl.pallas_call(kernel, out_shape=(pltpu.VMEM((rows, cols), jnp.float32),...  57.2 us

profile of v3, /device:TPU:1, one launch (start us, length us, event | category | flops | bytes accessed | tf_op | source)
XLA Modules:
  0.0 58.1 jit_solution(13244806285050468970)
XLA Ops:
  0.0 57.2 %shard_map.46 = (f32[512,512]{1,0:T(8,128)S(1)}, f32[1,512]{1,0:T(1,128)S(1)}) custom-call(bf16[512,512]{1,0:T(8,128)(2,1)} %v_hbm.1, s32[4,4]{1,0:T(4,128)} %tile_hbm.1, s32[4,4]{1,0:T(4,128)} %keep_hbm.1, s32[1,512]{1,0:T(1,128)} %bitcast.3), custom_call_target="tpu_custom_call" | custom-call | tf_op jit(solution)/shard_map/pallas_call | solution.py:474
  57.2 0.9 %multiply_convert_fusion = bf16[512,512]{1,0:T(8,128)(2,1)} fusion(f32[512,512]{1,0:T(8,128)S(1)} %get-tuple-element.7, f32[512]{0:T(512)S(1)} %bitcast.2), kind=kLoop, calls=%fused_computation | loop fusion | flops 524288 | bytes 1574912 | tf_op jit(solution)/shard_map/convert_element_type | solution.py:506

commit v4 on v3

--- a/solution.py
+++ b/solution.py
@@ -108,9 +108,9 @@
             device_id=neighbours[n],
         )
 
-    def z_copy(c, hop, n, sent=None):
+    def z_copy(c, hop, n, sent=None, lo=0, count=part):
         sign = 1 - 2 * n
-        spot = pl.ds(c * part, part)
+        spot = pl.ds(c * part + lo, count)
         to = sign * (hop + 1) % CHIPS
         return pltpu.make_async_remote_copy(
             src_ref=row_panel.at[sign * hop % CHIPS * CORES, spot],
@@ -137,6 +137,10 @@
                 @pl.when(z != CHIPS - 1)
                 def _():
                     z_copy(*DETOUR, 0, detour_send.at[0]).start()
+
+                @pl.when(z == CHIPS - 1)
+                def _():
+                    z_copy(*DETOUR, 0, detour_send.at[0], 0, part // 2).start()
             else:
                 z_copy(*Z_ORDER[n - 4][s], n - 4).start()
 
@@ -153,12 +157,12 @@
     stored = tile_ref[...].astype(jnp.float32)
     for q in range(CHUNKS):
         load(q).wait()
-        for lo in range(q * part, (q + 1) * part, min(part, TB)):
+        for lo in range(q * part, (q + 1) * part, TB):
             for b in range(cols // TB):
-                r, c = slice(lo, lo + min(part, TB)), slice(b * TB, (b + 1) * TB)
+                r, c = slice(lo, lo + TB), slice(b * TB, (b + 1) * TB)
                 i = lo // TB
-                factor = jnp.broadcast_to(stored[i : i + 1, b : b + 1], (min(part, TB), TB))
-                tile = (loaded[r, c].astype(jnp.float32) * factor).astype(jnp.bfloat16)
+                factor = jnp.broadcast_to(stored[i : i + 1, b : b + 1], (EXTRA, TB)).astype(jnp.bfloat16)
+                tile = loaded[r, c] * jnp.concatenate([factor] * (TB // EXTRA), axis=0)
                 row_panel[0, r, c] = tile
                 col_panel[r, c] = tile
 
@@ -284,6 +288,11 @@
             found = found + (i == k).astype(jnp.int32) * (value - values[0])
         return found
 
+    def met(of):
+        dz, side = of
+        k = (z - dz + CHIPS) % CHIPS * CORES + (core + side) % CORES
+        return (x - k // SIDE + SIDE) % SIDE * SIDE + (y - k % SIDE + SIDE) % SIDE
+
     def multiply(j, summed):
         dz, lane = inner(j)
         block = col_panel[pl.ds(pl.multiple_of(j * rows, rows), rows)]
@@ -318,13 +327,12 @@
             def _(i):
                 dz = pick(i, [c[0] for c in came])
                 side = pick(i, [c[1] for c in came])
-                k = (z - dz + CHIPS) % CHIPS * CORES + (core + side) % CORES
-                j = (x - k // SIDE + SIDE) % SIDE * SIDE + (y - k % SIDE + SIDE) % SIDE
-                met = j == old[0]
+                j = met((dz, side))
+                here = j == old[0]
                 for p in old[1:]:
-                    met = met | (j == p)
-
-                @pl.when(met)
+                    here = here | (j == p)
+
+                @pl.when(here)
                 def _():
                     multiply(j, step > SUMMED)
 
@@ -410,24 +418,32 @@
             if s == Z_AT[DETOUR[0], CHIPS - DETOUR[1]]:
                 @pl.when(z == 1)
                 def _():
-                    z_copy(*DETOUR, 1, detour_send.at[1]).start()
+                    z_copy(*DETOUR, 1, detour_send.at[1], part // 2, part // 2).start()
 
     with jax.named_scope("multiplyA"):
         compute(NEAR_AT[-1][0], before)
-    with jax.named_scope("pairlast"):
-        take_pair(CHIPS // 2)
-    with jax.named_scope("multiplyB"):
-        compute(NEAR_AT[-1][1], NEAR_AT[-1][0])
-
     masks[1].wait()
     masks[2].wait()
     kept = keep_ref[...].astype(jnp.float32)
     level = 0.125 * thr_ref[...].astype(jnp.float32)
-    with jax.named_scope("xy"):
-        take_xy(SLOTS - 1)
-    dz, lane = inner(LAST)
+    far = met((CHIPS // 2, 1))
+    for turn in range(CORES):
+        with jax.named_scope(f"last{turn}"):
+            @pl.when(core == turn)
+            def _():
+                take_pair(CHIPS // 2)
+
+            @pl.when(core != turn)
+            def _():
+                take_xy(SLOTS - 1)
+        if turn == 0:
+            @pl.when(far != LAST)
+            def _():
+                multiply((1 - core) * far + core * LAST, True)
+    final = core * far + (1 - core) * LAST
+    dz, lane = inner(final)
     slot = dz * CORES + lane
-    block = col_panel[LAST * rows : (LAST + 1) * rows]
+    block = col_panel[pl.ds(pl.multiple_of(final * rows, rows), rows)]
     lines = psum[...] + jnp.dot(row_panel[slot, rows:], block, preferred_element_type=jnp.float32)
     cut = level * ((lines[2:3] + lines[1:2] + lines[0:1]) / order)
     parts = [jnp.zeros((1, TB), jnp.float32) for _ in range(cols // TB)]
@@ -452,10 +468,10 @@
             device_id=neighbours[0],
         ).wait_send()
 
-    for n, sends in ((0, z != CHIPS - 1), (1, z == 1)):
+    for n, sends, count in ((0, z != CHIPS - 1, part), (0, z == CHIPS - 1, part // 2), (1, z == 1, part // 2)):
         @pl.when(sends)
         def _():
-            z_copy(*DETOUR, n, detour_send.at[n]).wait_send()
+            z_copy(*DETOUR, n, detour_send.at[n], 0, count).wait_send()
 
     with jax.named_scope("totals"):
         totals_all.wait_send()

time: 58.2 us -> 57.5 us (0.988)
  Pallas kernels: 57.2 us -> 56.4 us
    pallas_call x1, Pallas kernels: 57.2 us -> 56.4 us  [on_device(): pl.pallas_call(kernel, out_shape=(pltpu.VMEM((rows, cols), jnp.float32),...]
where the time goes in v4:
time: 57.5 us; the launch traced here: 57.4 us
  Pallas kernels  56.4 us (98%)
  other arithmetic  0.91 us (2%)
    pallas_call x1, Pallas kernels, on_device(): pl.pallas_call(kernel, out_shape=(pltpu.VMEM((rows, cols), jnp.float32),...  56.4 us

profile of v4, /device:TPU:1, one launch (start us, length us, event | category | flops | bytes accessed | tf_op | source)
XLA Modules:
  0.0 57.4 jit_solution(16958548132260569315)
XLA Ops:
  0.0 56.4 %shard_map.46 = (f32[512,512]{1,0:T(8,128)S(1)}, f32[1,512]{1,0:T(1,128)S(1)}) custom-call(bf16[512,512]{1,0:T(8,128)(2,1)} %v_hbm.1, s32[4,4]{1,0:T(4,128)} %tile_hbm.1, s32[4,4]{1,0:T(4,128)} %keep_hbm.1, s32[1,512]{1,0:T(1,128)} %bitcast.3), custom_call_target="tpu_custom_call" | custom-call | tf_op jit(solution)/shard_map/pallas_call | solution.py:490
  56.5 0.9 %multiply_convert_fusion = bf16[512,512]{1,0:T(8,128)(2,1)} fusion(f32[512,512]{1,0:T(8,128)S(1)} %get-tuple-element.7, f32[512]{0:T(512)S(1)} %bitcast.2), kind=kLoop, calls=%fused_computation | loop fusion | flops 524288 | bytes 1574912 | tf_op jit(solution)/shard_map/convert_element_type | solution.py:522

commit v5 on v4

--- a/solution.py
+++ b/solution.py
@@ -123,7 +123,8 @@
         spot = pl.ds(c * part, part)
         return pltpu.make_async_remote_copy(
             src_ref=row_panel.at[dz * CORES, spot], dst_ref=row_panel.at[dz * CORES + 1, spot],
-            send_sem=bulk_send.at[1], recv_sem=pair_recv.at[min(dz, CHIPS - dz)],
+            send_sem=bulk_send.at[1],
+            recv_sem=pair_recv.at[CHIPS // 2 + 1 if Z_AT.get((c, dz)) == Z_SLOTS - 1 else min(dz, CHIPS - dz)],
             device_id=neighbours[6],
         )
 
@@ -174,16 +175,17 @@
     for s in range(AHEAD - 1):
         for n in range(6):
             when_not(n, lambda: send(n, s))
-    for n in (6, 0, 2, 4, 1, 3, 5):
-        if n == 6:
-            when_not(n, lambda: [send(n, s) for s in range(CHUNKS)])
-
+    def open_late(n):
         @pl.when(later[n])
         def _():
             with jax.named_scope(f"open{n}"):
                 pl.semaphore_wait(ready.at[n], 1)
-            for s in range(CHUNKS if n == 6 else AHEAD - 1):
+            for s in range(CHUNKS if n == 6 else AHEAD - (n != 5)):
                 send(n, s)
+
+    when_not(6, lambda: [send(6, s) for s in range(CHUNKS)])
+    for n in (6, 0, 2, 4, 1, 3):
+        open_late(n)
 
     def greet(k, over):
         for device in neighbours[4 * over : 4 + 3 * over]:
@@ -193,7 +195,6 @@
         pl.semaphore_wait(hello.at[2 * over + k % 2], 4 - over)
 
     greet(0, 0)
-    greet(0, 1)
 
     def spread(buffer, k, count, device):
         def copy(d):
@@ -206,7 +207,10 @@
             src_ref=buffer.at[pl.ds(1, count - 1)], dst_ref=buffer.at[pl.ds(1, count - 1)],
             send_sem=small_send.at[0], recv_sem=small_recv.at[k], device_id=neighbours[6],
         )
-        return [copy(d) for d in range(1, count)], everything
+        def far(d):
+            return min(d // SIDE, SIDE - d // SIDE) + min(d % SIDE, SIDE - d % SIDE)
+
+        return [copy(d) for d in sorted(range(1, count), key=far, reverse=True)], everything
 
     def by_row(d):
         return xy_device(d // SIDE, d % SIDE)
@@ -230,8 +234,11 @@
                 greet(k + 1, 0)
     for copy in column_sums:
         copy.start()
-    for n in range(6):
+    for n in range(5):
         send(n, AHEAD - 1)
+    when_not(5, lambda: send(5, AHEAD - 1))
+    open_late(5)
+    greet(0, 1)
 
     block_sums, block_sums_all = spread(stats, 1, CHIPS, by_col)
 
@@ -293,48 +300,66 @@
         k = (z - dz + CHIPS) % CHIPS * CORES + (core + side) % CORES
         return (x - k // SIDE + SIDE) % SIDE * SIDE + (y - k % SIDE + SIDE) % SIDE
 
-    def multiply(j, summed):
-        dz, lane = inner(j)
-        block = col_panel[pl.ds(pl.multiple_of(j * rows, rows), rows)]
+    def multiply(blocks, summed):
+        term = None
+        for j in blocks:
+            dz, lane = inner(j)
+            left = row_panel[dz * CORES + lane] if summed else row_panel[dz * CORES + lane, :rows]
+            right = col_panel[pl.ds(pl.multiple_of(j * rows, rows), rows)]
+            one = jnp.dot(left, right, preferred_element_type=jnp.float32)
+            term = one if term is None else term + one
+        acc[...] += term[:rows]
         if summed:
-            term = jnp.dot(row_panel[dz * CORES + lane], block, preferred_element_type=jnp.float32)
-            acc[...] += term[:rows]
             psum[...] += term[rows:]
-        else:
-            acc[...] += jnp.dot(
-                row_panel[dz * CORES + lane, :rows], block, preferred_element_type=jnp.float32
-            )
+
+    def multiply_those(found, summed):
+        (first, one), (second, other) = found
+
+        @pl.when(one & other)
+        def _():
+            multiply((first, second), summed)
+
+        @pl.when(one ^ other)
+        def _():
+            multiply((jnp.where(one, first, second),), summed)
 
     def compute(step, before):
         fresh = [p for p in range(SIDE * SIDE) if p != LAST and before < BLOCK_AT[p] <= step]
-        assert before < step
-        if fresh:
+        if len(fresh) == 2:
+            multiply_those([(p, near(*inner(p), step)) for p in fresh], step > SUMMED)
+        elif fresh:
             @pl.loop(0, len(fresh))
             def _(i):
                 j = pick(i, fresh)
 
                 @pl.when(near(*inner(j), step))
                 def _():
-                    multiply(j, step > SUMMED)
+                    multiply((j,), step > SUMMED)
 
         old = [p for p in range(SIDE * SIDE) if p != LAST and BLOCK_AT[p] <= before]
         came = [
             (dz, side) for side in range(CORES) for h in range(CHIPS // 2 + 1)
             for dz in sorted({h, (CHIPS - h) % CHIPS}) if before < NEAR_AT[h][side] <= step
         ]
-        if old and came:
+        def there(of):
+            j = met(of)
+            here = j == old[0]
+            for p in old[1:]:
+                here = here | (j == p)
+            return j, here
+
+        if old and len(came) == 2:
+            multiply_those([there(of) for of in came], step > SUMMED)
+        elif old and came:
             @pl.loop(0, len(came))
             def _(i):
                 dz = pick(i, [c[0] for c in came])
                 side = pick(i, [c[1] for c in came])
-                j = met((dz, side))
-                here = j == old[0]
-                for p in old[1:]:
-                    here = here | (j == p)
+                j, here = there((dz, side))
 
                 @pl.when(here)
                 def _():
-                    multiply(j, step > SUMMED)
+                    multiply((j,), step > SUMMED)
 
     def add_sums(step):
         fresh = [p for p in range(SIDE * SIDE) if BLOCK_AT[p] <= step]
@@ -368,11 +393,16 @@
                     pair_copy(c, dz).start()
 
     def take_pair(h):
-        await_rows(len({h, -h % CHIPS}) * rows, pair_recv.at[h])
+        await_rows(rows // 2 if h >= CHIPS // 2 else rows if h == 0 else 2 * rows, pair_recv.at[h])
 
     before = -1
     for s in range(SLOTS - 1):
         if s < SLOTS - 1:
+            if s == Z_SLOTS - 1:
+                @pl.when(z != 0)
+                def _():
+                    with jax.named_scope(f"z{s}"):
+                        take_z(s)
             with jax.named_scope(f"xy{s}"):
                 take_xy(s)
             for n in range(4):
@@ -388,7 +418,8 @@
                 with jax.named_scope(f"pair{h}"):
                     take_pair(h)
         if s == Z_SLOTS - 1:
-            with jax.named_scope(f"z{s}"):
+            @pl.when(z == 0)
+            def _():
                 take_z(s)
         with jax.named_scope(f"sums{s}"):
             if s < 3:
@@ -432,6 +463,8 @@
             @pl.when(core == turn)
             def _():
                 take_pair(CHIPS // 2)
+                if turn == 0:
+                    take_pair(CHIPS // 2 + 1)
 
             @pl.when(core != turn)
             def _():
@@ -439,7 +472,7 @@
         if turn == 0:
             @pl.when(far != LAST)
             def _():
-                multiply((1 - core) * far + core * LAST, True)
+                multiply(((1 - core) * far + core * LAST,), True)
     final = core * far + (1 - core) * LAST
     dz, lane = inner(final)
     slot = dz * CORES + lane
@@ -447,7 +480,14 @@
     lines = psum[...] + jnp.dot(row_panel[slot, rows:], block, preferred_element_type=jnp.float32)
     cut = level * ((lines[2:3] + lines[1:2] + lines[0:1]) / order)
     parts = [jnp.zeros((1, TB), jnp.float32) for _ in range(cols // TB)]
-    for lo in range(0, rows, TB):
+    late = sorted(c for c in range(CHUNKS) if Z_AT[c, CHIPS // 2] == Z_SLOTS - 1)
+    for q in sorted(range(CHUNKS), key=lambda c: c in late):
+        if q == late[0]:
+            with jax.named_scope("last2"):
+                @pl.when(core == 1)
+                def _():
+                    take_pair(CHIPS // 2 + 1)
+        lo = q * TB
         term = jnp.dot(row_panel[slot, lo : lo + TB], block, preferred_element_type=jnp.float32)
         for b in range(cols // TB):
             r, c = slice(lo, lo + TB), slice(b * TB, (b + 1) * TB)
@@ -506,7 +546,7 @@
             dma((2,)),
             dma((SLOTS,)),
             dma((Z_SLOTS,)),
-            dma((CHIPS // 2 + 1,)),
+            dma((CHIPS // 2 + 2,)),
             dma((2,)),
             dma((1,)),
             dma((4,)),

time: 57.5 us -> 57.1 us (level)
  no operation moved by 1% of the time
where the time goes in v5:
time: 57.1 us; the launch traced here: 57 us
  Pallas kernels  56.1 us (98%)
  other arithmetic  0.91 us (2%)
    pallas_call x1, Pallas kernels, on_device(): pl.pallas_call(kernel, out_shape=(pltpu.VMEM((rows, cols), jnp.float32),...  56.1 us

profile of v5, /device:TPU:1, one launch (start us, length us, event | category | flops | bytes accessed | tf_op | source)
XLA Modules:
  0.0 57.0 jit_solution(3386644435120202708)
XLA Ops:
  0.0 56.1 %shard_map.46 = (f32[512,512]{1,0:T(8,128)S(1)}, f32[1,512]{1,0:T(1,128)S(1)}) custom-call(bf16[512,512]{1,0:T(8,128)(2,1)} %v_hbm.1, s32[4,4]{1,0:T(4,128)} %tile_hbm.1, s32[4,4]{1,0:T(4,128)} %keep_hbm.1, s32[1,512]{1,0:T(1,128)} %bitcast.3), custom_call_target="tpu_custom_call" | custom-call | tf_op jit(solution)/shard_map/pallas_call | solution.py:530
  56.1 0.9 %multiply_convert_fusion = bf16[512,512]{1,0:T(8,128)(2,1)} fusion(f32[512,512]{1,0:T(8,128)S(1)} %get-tuple-element.7, f32[512]{0:T(512)S(1)} %bitcast.2), kind=kLoop, calls=%fused_computation | loop fusion | flops 524288 | bytes 1574912 | tf_op jit(solution)/shard_map/convert_element_type | solution.py:562

commit v6 on v5

--- a/solution.py
+++ b/solution.py
@@ -141,7 +141,7 @@
 
                 @pl.when(z == CHIPS - 1)
                 def _():
-                    z_copy(*DETOUR, 0, detour_send.at[0], 0, part // 2).start()
+                    z_copy(*DETOUR, 0, detour_send.at[0], 0, 32).start()
             else:
                 z_copy(*Z_ORDER[n - 4][s], n - 4).start()
 
@@ -399,10 +399,8 @@
     for s in range(SLOTS - 1):
         if s < SLOTS - 1:
             if s == Z_SLOTS - 1:
-                @pl.when(z != 0)
-                def _():
-                    with jax.named_scope(f"z{s}"):
-                        take_z(s)
+                with jax.named_scope(f"z{s}"):
+                    take_z(s)
             with jax.named_scope(f"xy{s}"):
                 take_xy(s)
             for n in range(4):
@@ -417,10 +415,6 @@
             if s == NEAR_AT[h][1]:
                 with jax.named_scope(f"pair{h}"):
                     take_pair(h)
-        if s == Z_SLOTS - 1:
-            @pl.when(z == 0)
-            def _():
-                take_z(s)
         with jax.named_scope(f"sums{s}"):
             if s < 3:
                 greeted(s, 1)
@@ -449,10 +443,14 @@
             if s == Z_AT[DETOUR[0], CHIPS - DETOUR[1]]:
                 @pl.when(z == 1)
                 def _():
-                    z_copy(*DETOUR, 1, detour_send.at[1], part // 2, part // 2).start()
-
+                    z_copy(*DETOUR, 1, detour_send.at[1], 32, part - 32).start()
+
+    near_last = met((CHIPS // 2, 0))
     with jax.named_scope("multiplyA"):
-        compute(NEAR_AT[-1][0], before)
+        @pl.when((core == 1) & (near_last != LAST))
+        def _():
+            multiply((near_last,), True)
+
     masks[1].wait()
     masks[2].wait()
     kept = keep_ref[...].astype(jnp.float32)
@@ -470,9 +468,10 @@
             def _():
                 take_xy(SLOTS - 1)
         if turn == 0:
-            @pl.when(far != LAST)
-            def _():
-                multiply(((1 - core) * far + core * LAST,), True)
+            multiply_those([
+                (near_last, (core == 0) & (near_last != LAST)),
+                ((1 - core) * far + core * LAST, far != LAST),
+            ], True)
     final = core * far + (1 - core) * LAST
     dz, lane = inner(final)
     slot = dz * CORES + lane
@@ -508,7 +507,7 @@
             device_id=neighbours[0],
         ).wait_send()
 
-    for n, sends, count in ((0, z != CHIPS - 1, part), (0, z == CHIPS - 1, part // 2), (1, z == 1, part // 2)):
+    for n, sends, count in ((0, z != CHIPS - 1, part), (0, z == CHIPS - 1, 32), (1, z == 1, part - 32)):
         @pl.when(sends)
         def _():
             z_copy(*DETOUR, n, detour_send.at[n], 0, count).wait_send()

time: 57.1 us -> 56.7 us (level)
  no operation moved by 1% of the time
where the time goes in v6:
time: 56.7 us; the launch traced here: 56.6 us
  Pallas kernels  55.7 us (98%)
  other arithmetic  0.91 us (2%)
    pallas_call x1, Pallas kernels, on_device(): pl.pallas_call(kernel, out_shape=(pltpu.VMEM((rows, cols), jnp.float32),...  55.7 us

profile of v6, /device:TPU:1, one launch (start us, length us, event | category | flops | bytes accessed | tf_op | source)
XLA Modules:
  0.0 56.6 jit_solution(6656581845630012653)
XLA Ops:
  0.0 55.7 %shard_map.46 = (f32[512,512]{1,0:T(8,128)S(1)}, f32[1,512]{1,0:T(1,128)S(1)}) custom-call(bf16[512,512]{1,0:T(8,128)(2,1)} %v_hbm.1, s32[4,4]{1,0:T(4,128)} %tile_hbm.1, s32[4,4]{1,0:T(4,128)} %keep_hbm.1, s32[1,512]{1,0:T(1,128)} %bitcast.3), custom_call_target="tpu_custom_call" | custom-call | tf_op jit(solution)/shard_map/pallas_call | solution.py:529
  55.7 0.9 %multiply_convert_fusion = bf16[512,512]{1,0:T(8,128)(2,1)} fusion(f32[512,512]{1,0:T(8,128)S(1)} %get-tuple-element.7, f32[512]{0:T(512)S(1)} %bitcast.2), kind=kLoop, calls=%fused_computation | loop fusion | flops 524288 | bytes 1574912 | tf_op jit(solution)/shard_map/convert_element_type | solution.py:561

commit v7 on v6

--- a/solution.py
+++ b/solution.py
@@ -73,17 +73,6 @@
     def z_device(dz, lane=0):
         return {"col": (z + dz + CHIPS) % CHIPS * CORES + (core if lane == 0 else 1 - core)}
 
-    neighbours = [xy_device(*link) for link in LINKS] + [z_device(1), z_device(-1), z_device(0, 1)]
-    later = [x < SIDE - 1, x == 0, y < SIDE - 1, y == 0, z < CHIPS - 1, z == 0, core == 1]
-    barrier = pltpu.get_barrier_semaphore()
-    earlier = 0
-    for n, device in enumerate(neighbours):
-        earlier = earlier + 1 - later[n].astype(jnp.int32)
-
-        @pl.when(later[n])
-        def _():
-            pl.semaphore_signal(barrier, inc=1, device_id=device)
-
     def load(q):
         spot = pl.ds(q * part, part)
         return pltpu.make_async_copy(v_hbm.at[spot], loaded.at[spot], load_sem.at[q])
@@ -98,6 +87,18 @@
         load(q).start()
     masks[1].start()
     masks[2].start()
+
+    neighbours = [xy_device(*link) for link in LINKS] + [z_device(1), z_device(-1), z_device(0, 1)]
+    later = [x < SIDE - 1, x == 0, y < SIDE - 1, y == 0, z < CHIPS - 1, z == 0, core == 1]
+    barrier = pltpu.get_barrier_semaphore()
+    earlier = 0
+    for n, device in enumerate(neighbours):
+        earlier = earlier + 1 - later[n].astype(jnp.int32)
+
+        @pl.when(later[n])
+        def _():
+            pl.semaphore_signal(barrier, inc=1, device_id=device)
+
 
     def xy_copy(c, place, n):
         to = shift(place, n)

time: 56.7 us -> 56.7 us (level)
  no operation moved by 1% of the time
where the time goes in v7:
time: 56.7 us; the launch traced here: 56.6 us
  Pallas kernels  55.7 us (98%)
  other arithmetic  0.91 us (2%)
    pallas_call x1, Pallas kernels, on_device(): pl.pallas_call(kernel, out_shape=(pltpu.VMEM((rows, cols), jnp.float32),...  55.7 us

profile of v7, /device:TPU:1, one launch (start us, length us, event | category | flops | bytes accessed | tf_op | source)
XLA Modules:
  0.0 56.6 jit_solution(15009708964650937155)
XLA Ops:
  0.0 55.7 %shard_map.46 = (f32[512,512]{1,0:T(8,128)S(1)}, f32[1,512]{1,0:T(1,128)S(1)}) custom-call(bf16[512,512]{1,0:T(8,128)(2,1)} %v_hbm.1, s32[4,4]{1,0:T(4,128)} %tile_hbm.1, s32[4,4]{1,0:T(4,128)} %keep_hbm.1, s32[1,512]{1,0:T(1,128)} %bitcast.3), custom_call_target="tpu_custom_call" | custom-call | tf_op jit(solution)/shard_map/pallas_call | solution.py:530
  55.7 0.9 %multiply_convert_fusion = bf16[512,512]{1,0:T(8,128)(2,1)} fusion(f32[512,512]{1,0:T(8,128)S(1)} %get-tuple-element.7, f32[512]{0:T(512)S(1)} %bitcast.2), kind=kLoop, calls=%fused_computation | loop fusion | flops 524288 | bytes 1574912 | tf_op jit(solution)/shard_map/convert_element_type | solution.py:562
